TPU v7x, 256 devices: a 2x2x32 block of a 4x8x32 slice. The times are simulated.
256 devices in a mesh: groups: 4 (over x, y), ep: 64 (over z, core).
Axes of the slice: x: 2, y: 2, z: 32, core: 2. Of those that a mesh axis runs over, the one named last changes fastest.
The devices are a block of a 4x8x32 slice.
Arguments:
- tokens: bfloat16 [16384, 2880], P(('groups', 'ep')), parts along dimension 0, may hold values from -6 to 6
- routes: int32 [16384, 4], P(('groups', 'ep')), parts along dimension 0, may hold values from 0 to 15, all different within a row; in each aligned block of 64 rows (0 to 63, 64 to 127, ...) at most 20 rows name the same one
- norm_gain: bfloat16 [2880], replicated, may hold values from 0.25 to 1.75
- router_weight: bfloat16 [2880, 16], replicated, may hold values from -0.02734375 to 0.02734375
- gate_up_weight: bfloat16 [64, 2880, 720], P('ep'), may hold values from -0.109375 to 0.109375
- down_weight: bfloat16 [64, 360, 2880], P('ep'), may hold values from -0.15625 to 0.15625
Outputs:
- mixed: bfloat16 [16384, 2880], P(('groups', 'ep')), parts along dimension 0
There are 4 independent parts, one for each index of `groups`. A program takes and returns all parts, laid end to end along the dimension named above; an argument that names none is the same for every part. Nothing has to cross between parts.
Inputs may be any that keep to these rules, and one draw needn't show every extreme that they name: `routes`: in each aligned block of 64 rows (the rows of one device), no expert is named by more than 20 rows; in some blocks one expert is named by exactly 20 rows. A row names 4 different experts.
All inputs are finite; a program needn't handle non-finite values.
Results may differ from a plain program's by a relative error of at most 0.005.
Values may be sent and summed in bfloat16 or wider, within the bound.
A program may use at most 128 MiB of HBM per device.

v0:
```python
import jax
import jax.numpy as jnp
from jax import lax
from jax.sharding import Mesh
from jax.sharding import PartitionSpec as P

EP = ("ep_0", "ep_1")
GROUPS_EP = ("groups", "ep_0", "ep_1")


def cut_along(array, dim, count):
    before, after = (array.shape[:dim], array.shape[dim + 1 :])
    return jnp.moveaxis(array.reshape(*before, count, -1, *after), dim, 0)


def laid_out(tiles, dim):
    shape = list(tiles.shape[1:])
    shape[dim] *= tiles.shape[0]
    return jnp.moveaxis(tiles, 0, dim).reshape(shape)


def exchange_in_order(tiles, axes, sequence):
    shape = [lax.axis_size(a) for a in axes]
    tiles = tiles.reshape(*shape, *tiles.shape[1:])
    for k in sequence:
        tiles = lax.all_to_all(tiles, axes[k], split_axis=k, concat_axis=k, tiled=True)
    return tiles.reshape(-1, *tiles.shape[len(axes) :])


def core_and_chips(array, groups, sequence, split_dim, concat_dim):
    count = lax.axis_size(groups[0]) * lax.axis_size(groups[1])
    tiles = cut_along(array, split_dim, count)
    return laid_out(exchange_in_order(tiles, groups, sequence), concat_dim)


def from_partner(array, axis, bit):
    return lax.ppermute(array, axis, [(i, i ^ 1 << bit) for i in range(lax.axis_size(axis))])


def shards(tokens, routes, norm_gain, router_weight, gate_up_weight, down_weight):
    tok_rows = tokens.shape[0]
    model_width = tokens.shape[1]
    top_count = routes.shape[1]
    experts = router_weight.shape[1]
    devices = lax.axis_size(EP)
    shard_count = devices // experts
    ff_dev = down_weight.shape[1]
    capacity = min(
        tok_rows, shard_count * (17 * tok_rows * top_count // (16 * experts * shard_count) + 1)
    )
    piece_rows = capacity // shard_count
    my_index = lax.axis_index(EP)
    stream = tokens.astype(jnp.float32)
    mean_square = jnp.mean(stream * stream, axis=-1, keepdims=True)
    normed = (stream * lax.rsqrt(mean_square + 1e-05) * norm_gain.astype(jnp.float32)).astype(
        jnp.bfloat16
    )
    logits = jnp.dot(normed, router_weight, preferred_element_type=jnp.float32)
    expert_ids = lax.broadcasted_iota(jnp.int32, (1, 1, experts), 2)
    onehot = routes[:, :, None] == expert_ids
    chosen = jnp.sum(jnp.where(onehot, logits[:, None, :], jnp.float32(0.0)), axis=-1)
    expo = jnp.exp(chosen)
    route_prob = expo / jnp.sum(expo, axis=-1, keepdims=True)
    flat_hits = onehot.astype(jnp.int32).reshape(tok_rows * top_count, experts)
    rank_before = jnp.cumsum(flat_hits, axis=0) - flat_hits
    slot_index = jnp.sum(flat_hits * rank_before, axis=1)
    position = routes.reshape(-1) * capacity + slot_index
    slot_iota = lax.broadcasted_iota(jnp.int32, (1, experts * capacity), 1)
    placement = position[:, None] == slot_iota
    selector = (
        placement.astype(jnp.bfloat16).reshape(tok_rows, top_count, experts * capacity).sum(axis=1)
    )
    combine_weight = jnp.where(placement, route_prob.reshape(-1)[:, None], jnp.float32(0.0))
    combine_weight = combine_weight.reshape(tok_rows, top_count, experts * capacity).sum(axis=1)
    buffer = jnp.einsum("te,td->ed", selector, normed, preferred_element_type=jnp.float32).astype(
        jnp.bfloat16
    )
    buffer = buffer.reshape(experts, capacity, model_width)
    outgoing = buffer.reshape(devices, piece_rows, model_width)
    received = core_and_chips(outgoing, ("ep_0", "ep_1"), (1, 0), 0, 0)
    for level in range(shard_count.bit_length() - 1):
        partner = from_partner(received, EP, level)
        upper = my_index >> level & 1 == 1
        received = jnp.where(
            upper,
            jnp.concatenate([partner, received], axis=1),
            jnp.concatenate([received, partner], axis=1),
        )
    rows_in = received.reshape(devices * capacity, model_width)
    hidden = jnp.dot(rows_in, gate_up_weight[0], preferred_element_type=jnp.float32)
    gate_part = hidden[:, :ff_dev]
    up_part = hidden[:, ff_dev:]
    activated = ((up_part + 1.0) * gate_part * jax.nn.sigmoid(1.702 * gate_part)).astype(
        jnp.bfloat16
    )
    partial_value = jnp.dot(activated, down_weight[0], preferred_element_type=jnp.float32).astype(
        jnp.bfloat16
    )
    partial_value = partial_value.reshape(devices, capacity, model_width)
    half_rows = capacity // 2
    upper_first = my_index >> 1 & 1 == 1
    lower_half = partial_value[:, :half_rows]
    upper_half = partial_value[:, half_rows:]
    kept = jnp.where(upper_first, upper_half, lower_half)
    sent = jnp.where(upper_first, lower_half, upper_half)
    arrived = from_partner(sent, EP, 1)
    summed = kept.astype(jnp.float32) + arrived.astype(jnp.float32)
    upper_second = my_index & 1 == 1
    lower_quarter = summed[:, :piece_rows]
    upper_quarter = summed[:, piece_rows:]
    kept_quarter = jnp.where(upper_second, upper_quarter, lower_quarter)
    sent_quarter = jnp.where(upper_second, lower_quarter, upper_quarter)
    arrived_quarter = from_partner(sent_quarter.astype(jnp.bfloat16), EP, 0).astype(
        sent_quarter.dtype
    )
    quarter_sum = kept_quarter + arrived_quarter
    returned = lax.all_to_all(
        quarter_sum.astype(jnp.bfloat16), EP, split_axis=0, concat_axis=0, tiled=True
    ).astype(quarter_sum.dtype)
    expert_sum = returned.reshape(experts, capacity, model_width)
    expert_sum = expert_sum.reshape(experts * capacity, model_width)
    mixture = jnp.dot(
        combine_weight,
        expert_sum,
        precision=lax.Precision.HIGHEST,
        preferred_element_type=jnp.float32,
    )
    return (stream + mixture).astype(jnp.bfloat16)


def solution(mesh):
    split = Mesh(mesh.devices.reshape(mesh.shape["groups"], 32, 2), ("groups", "ep_0", "ep_1"))
    placed = (
        P(GROUPS_EP, None),
        P(GROUPS_EP, None),
        P(),
        P(),
        P(EP, None, None),
        P(EP, None, None),
    )
    return jax.shard_map(
        shards, mesh=split, in_specs=placed, out_specs=P(GROUPS_EP, None), check_vma=False
    )
```

profile of v0, /device:TPU:46, one launch (start us, length us, event | category | flops | bytes accessed | tf_op | source)
XLA Modules:
  0.0 814.8 jit_solution(11306621285948052571)
XLA Ops:
  0.0 0.9 copy.76
  0.9 0.1 eq.61
  1.0 0.1 eq.57
  1.2 0.6 reduce-window.6
  1.7 0.2 slice_reduce_fusion
  2.0 0.1 fusion.20
  2.1 0.1 reduce_sum.60
  2.2 0.1 copy.79
  2.2 0.7 multiply_add_fusion
  2.9 0.1 fusion.14
  3.1 0.7 convert_element_type.54
  3.8 1.2 fusion.10
  4.9 3.0 convolution_convert_fusion.1
  7.9 4.2 reshape_reshape_reshape_reshape.3
  12.1 2.2 copy.80
  14.4 5.3 all_to_all.15
  19.6 1.5 copy.81
  21.1 212.7 %all_to_all.16 = bf16[32,2,1,5,2880]{4,1,3,2,0:T(2,128)(2,1)S(1)} all-to-all(bf16[32,2,1,5,2880]{4,1,3,2,0:T(2,128)(2,1)S(1)} %copy.81), channel_id=1, replica_groups=mesh['groups'=4,'ep_0'=32,'ep_1'=2] {'ep_0'}, dimensions={0} | all-to-all | bytes 3686400 | tf_op jit(solution)/shard_map/all_to_all | solution.py:26
  233.7 2.6 copy.82
  236.3 5.0 reshape_reshape.6
  241.3 4.2 collective-permute-done
  245.5 5.0 maximum_select_fusion.1
  250.5 0.0 collective-permute-start.1
  250.5 83.8 %collective-permute-done.1 = bf16[64,10,2880]{2,0,1:T(8,128)(2,1)} collective-permute-done((bf16[64,10,2880]{2,0,1:T(8,128)(2,1)}, bf16[64,10,2880]{2,0,1:T(8,128)(2,1)}, u32[]{:S(2)}, u32[]{:S(2)}) %collective-permute-start.1) | collective-permute-done | bytes 3686432 | tf_op jit(solution)/shard_map/ppermute | solution.py:37
  334.3 8.7 %maximum_select_fusion = bf16[64,20,2880]{2,0,1:T(8,128)(2,1)} fusion(bf16[64,10,2880]{2,0,1:T(8,128)(2,1)} %maximum_select_fusion.1, bf16[64,10,2880]{2,0,1:T(8,128)(2,1)} %collective-permute-done.1, pred[]{:T(512)S(6)} %eq.72), kind=kLoop, calls=%fused_computation.1 | loop fusion | flops 11059200 | bytes 14745601 | tf_op jit(solution)/shard_map/jit(_where)/select_n | solution.py:84
  343.1 10.8 %copy.83 = bf16[64,20,2880]{2,1,0:T(8,128)(2,1)} copy(bf16[64,20,2880]{2,0,1:T(8,128)(2,1)} %maximum_select_fusion) | data formatting | bytes 14745600 | tf_op jit(solution)/shard_map/jit(_where)/select_n | solution.py:84
  353.9 11.7 %select_n.65 = bf16[1280,2880]{1,0:T(8,128)(2,1)} reshape(bf16[64,20,2880]{2,1,0:T(8,128)(2,1)} %copy.83) | data formatting | bytes 14745600 | tf_op jit(solution)/shard_map/jit(_where)/select_n | solution.py:84
  365.6 9.9 %fusion = f32[1280,720]{0,1:T(8,128)S(1)} fusion(bf16[1280,2880]{1,0:T(8,128)(2,1)} %select_n.65, bf16[1,2880,720]{1,2,0:T(8,128)(2,1)} %param.10), kind=kOutput, calls=%fused_computation.3 | convolution fusion | flops 5308416000 | bytes 15206400 | tf_op jit(solution)/shard_map/dot_general | solution.py:90
  375.6 6.7 convolution_convert_fusion
  382.3 10.3 %copy.84 = bf16[1280,2880]{1,0:T(8,128)(2,1)} copy(bf16[1280,2880]{0,1:T(8,128)(2,1)} %convolution_convert_fusion) | data formatting | bytes 14745600 | tf_op jit(solution)/shard_map/convert_element_type | solution.py:96
  392.7 11.9 %reshape.88 = bf16[64,20,2880]{2,1,0:T(8,128)(2,1)} reshape(bf16[1280,2880]{1,0:T(8,128)(2,1)} %copy.84) | data formatting | bytes 14745600 | tf_op jit(solution)/shard_map/reshape | solution.py:99
  404.6 11.0 %fusion.24 = (bf16[64,10,2880]{2,1,0:T(8,128)(2,1)}, bf16[64,10,2880]{2,1,0:T(8,128)(2,1)}) fusion(bf16[64,20,2880]{2,1,0:T(8,128)(2,1)} %reshape.88), kind=kLoop, calls=%fused_computation.46 | loop fusion | bytes 14745600 | tf_op jit(solution)/shard_map/slice | solution.py:103
  415.6 8.5 %broadcast_select_fusion = bf16[64,10,2880]{2,0,1:T(8,128)(2,1)} fusion(pred[]{:T(512)S(6)} %eq.72, bf16[64,10,2880]{2,1,0:T(8,128)(2,1)} %get-tuple-element.6, bf16[64,10,2880]{2,1,0:T(8,128)(2,1)} %get-tuple-element.5), kind=kLoop, calls=%fused_computation.9 | loop fusion | flops 1843200 | bytes 11059201 | tf_op jit(solution)/shard_map/jit(_where)/select_n | solution.py:105
  424.1 0.3 collective-permute-start.2
  424.4 82.7 %collective-permute-done.2 = bf16[64,10,2880]{2,0,1:T(8,128)(2,1)} collective-permute-done((bf16[64,10,2880]{2,0,1:T(8,128)(2,1)}, bf16[64,10,2880]{2,0,1:T(8,128)(2,1)}, u32[]{:S(2)}, u32[]{:S(2)}) %collective-permute-start.2) | collective-permute-done | bytes 3686432 | tf_op jit(solution)/shard_map/ppermute | solution.py:37
  507.0 7.1 convert_add_fusion
  514.1 0.3 select_convert_fusion
  514.5 0.1 collective-permute-start.3
  514.6 3.8 collective-permute-done.3
  518.4 0.5 add_convert_fusion
  519.0 2.7 copy.87
  521.7 7.4 all-to-all-start.2
  529.1 0.3 fusion.16
  529.5 0.0 copy-start.1
  529.5 0.1 select_reduce_fusion
  529.6 277.3 %all-to-all-done.2 = bf16[64,5,2880]{2,1,0:T(8,128)(2,1)} async-done(((bf16[64,5,2880]{2,1,0:T(8,128)(2,1)}), bf16[64,5,2880]{2,1,0:T(8,128)(2,1)}, u32[]{:S(2)}, u32[]{:S(2)}) %all-to-all-start.2) | async-done | bytes 1843232 | tf_op jit(solution)/shard_map/all_to_all | solution.py:117
  806.9 4.5 reshape_reshape.7
  811.5 3.4 fusion.2
  (17 shorter events, 0.1 us)
Async XLA Ops:
  0.0 375.6 %copy-start = (bf16[1,360,2880]{2,1,0:T(8,128)(2,1)S(1)}, bf16[1,360,2880]{2,1,0:T(8,128)(2,1)}, u32[]{:S(2)}) copy-start(bf16[1,360,2880]{2,1,0:T(8,128)(2,1)} %param.11) | copy-start | bytes 6220804
  241.3 4.2 collective-permute-start
  250.5 83.8 %collective-permute-start.1 = (bf16[64,10,2880]{2,0,1:T(8,128)(2,1)}, bf16[64,10,2880]{2,0,1:T(8,128)(2,1)}, u32[]{:S(2)}, u32[]{:S(2)}) collective-permute-start(bf16[64,10,2880]{2,0,1:T(8,128)(2,1)} %maximum_select_fusion.1), channel_id=1, source_target_pairs={{0,2},{1,3},{2,0},{3,1},{4,6},{5,7},{6,4},{7,5},{8,10},{9,11},{10,... | collective-permute-start | bytes 11059208 | tf_op jit(solution)/shard_map/ppermute | solution.py:37
  424.1 82.9 %collective-permute-start.2 = (bf16[64,10,2880]{2,0,1:T(8,128)(2,1)}, bf16[64,10,2880]{2,0,1:T(8,128)(2,1)}, u32[]{:S(2)}, u32[]{:S(2)}) collective-permute-start(bf16[64,10,2880]{2,0,1:T(8,128)(2,1)} %broadcast_select_fusion), channel_id=1, source_target_pairs={{0,2},{1,3},{2,0},{3,1},{4,6},{5,7},{6,4},{7,5},{8,10},{9,11},{10,... | collective-permute-start | bytes 11059208 | tf_op jit(solution)/shard_map/ppermute | solution.py:37
  514.5 4.0 collective-permute-start.3
  521.7 7.4 copy-start.2
  521.7 7.4 copy-start.4
  521.7 7.7 copy-start.3
  521.7 285.2 %all-to-all-start.2 = ((bf16[64,5,2880]{2,1,0:T(8,128)(2,1)}), bf16[64,5,2880]{2,1,0:T(8,128)(2,1)}, u32[]{:S(2)}, u32[]{:S(2)}) async-start(bf16[64,5,2880]{2,1,0:T(8,128)(2,1)} %copy.87), calls=%async_computation.2 | async-start | bytes 6029312 | tf_op jit(solution)/shard_map/all_to_all | solution.py:117
  529.5 285.4 %copy-start.1 = (bf16[1,360,2880]{2,1,0:T(8,128)(2,1)S(1)}, bf16[1,360,2880]{2,1,0:T(8,128)(2,1)}, u32[]{:S(2)}) copy-start(bf16[1,360,2880]{2,1,0:T(8,128)(2,1)} %param.11) | copy-start | bytes 6220804
where the time goes:
time: 816 us; the launch traced here: 815 us
  waiting for transfers between devices  452 us (55%)
  blocking collectives  218 us (27%)
  local copies, waits for them, and re-layouts  80.1 us (10%)
  other arithmetic  33.8 us (4%)
  matrix products  23.3 us (3%)
    all_to_all x1, waiting for transfers between devices, shards(): lax.all_to_all(quarter_sum.astype(jnp.bfloat16), EP, split_axis=0, concat...  277 us
    all_to_all x2, blocking collectives, exchange_in_order(): lax.all_to_all(tiles, axes[k], split_axis=k, concat_axis=k, tiled=True)  218 us
    ppermute x4, waiting for transfers between devices, from_partner(): lax.ppermute(array, axis, [(i, i ^ 1 << bit) for i in range(lax.axis_size...  174 us
    select_n x2, local copies, waits for them, and re-layouts, shards(): jnp.where(upper, jnp.concatenate([partner, received], axis=1), jnp.concat...  22.6 us
  transfers between devices with their start and end apart: 5, of which 5 were waited for; matrix products, arithmetic and copies ran while one was open for 0% of the time, Pallas kernels for 0%

commit v1 on v0

v1 whole, which is shorter than its diff:
```python
import jax
import jax.numpy as jnp
from jax import lax
from jax.sharding import Mesh
from jax.sharding import PartitionSpec as P

EP = ("ep_0", "ep_1")
GROUPS_EP = ("groups", "ep_0", "ep_1")


def shards(tokens, routes, norm_gain, router_weight, gate_up_weight, down_weight):
    experts = router_weight.shape[1]
    devices = lax.axis_size(EP)
    shard_count = devices // experts
    ff_dev = down_weight.shape[1]
    stream = tokens.astype(jnp.float32)
    mean_square = jnp.mean(stream * stream, axis=-1, keepdims=True)
    normed = (stream * lax.rsqrt(mean_square + 1e-05) * norm_gain.astype(jnp.float32)).astype(
        jnp.bfloat16
    )
    rows_in = lax.all_gather(normed, EP, axis=0, tiled=True)
    logits = jnp.dot(normed, router_weight, preferred_element_type=jnp.float32)
    expert_ids = lax.broadcasted_iota(jnp.int32, (1, 1, experts), 2)
    onehot = routes[:, :, None] == expert_ids
    chosen = jnp.sum(jnp.where(onehot, logits[:, None, :], jnp.float32(0.0)), axis=-1)
    expo = jnp.exp(chosen)
    route_prob = expo / jnp.sum(expo, axis=-1, keepdims=True)
    weight = jnp.sum(jnp.where(onehot, route_prob[:, :, None], jnp.float32(0.0)), axis=1)
    weights = lax.all_gather(weight.T, EP, axis=1, tiled=True)
    my_expert = lax.axis_index(EP) // shard_count
    mine = lax.dynamic_slice_in_dim(weights, my_expert, 1, axis=0).reshape(-1, 1)
    hidden = jnp.dot(rows_in, gate_up_weight[0], preferred_element_type=jnp.float32)
    gate_part = hidden[:, :ff_dev]
    up_part = hidden[:, ff_dev:]
    activated = ((up_part + 1.0) * gate_part * jax.nn.sigmoid(1.702 * gate_part)).astype(
        jnp.bfloat16
    )
    partial_value = jnp.dot(activated, down_weight[0], preferred_element_type=jnp.float32)
    share = jnp.where(mine != 0.0, partial_value * mine, jnp.float32(0.0)).astype(jnp.bfloat16)
    mixture = lax.psum_scatter(share, EP, scatter_dimension=0, tiled=True)
    return (stream + mixture.astype(jnp.float32)).astype(jnp.bfloat16)


def solution(mesh):
    split = Mesh(mesh.devices.reshape(mesh.shape["groups"], 32, 2), ("groups", "ep_0", "ep_1"))
    placed = (
        P(GROUPS_EP, None),
        P(GROUPS_EP, None),
        P(),
        P(),
        P(EP, None, None),
        P(EP, None, None),
    )
    return jax.shard_map(
        shards, mesh=split, in_specs=placed, out_specs=P(GROUPS_EP, None), check_vma=False
    )
```

time: 816 us -> 476 us (0.58)
  blocking collectives: 218 us -> 78 us
  waiting for transfers between devices: 452 us -> 330 us
  local copies, waits for them, and re-layouts: 80.1 us -> 0.39 us
  other arithmetic: 33.8 us -> 7.22 us
  matrix products: 23.3 us -> 46.7 us
  between operations: 0.16 us -> 13.5 us
    all_to_all x1 -> x0, waiting for transfers between devices: 277 us -> none  [shards(): lax.all_to_all(quarter_sum.astype(jnp.bfloat16), EP, split_axis=0, concat...]
    reduce_scatter x0 -> x1, waiting for transfers between devices: none -> 238 us  [shards(): mixture = lax.psum_scatter(share, EP, scatter_dimension=0, tiled=True)]
    all_to_all x2 -> x0, blocking collectives: 218 us -> none  [exchange_in_order(): lax.all_to_all(tiles, axes[k], split_axis=k, concat_axis=k, tiled=True)]
    ppermute x4 -> x0, waiting for transfers between devices: 174 us -> none  [from_partner(): lax.ppermute(array, axis, [(i, i ^ 1 << bit) for i in range(lax.axis_size...]
    all_gather x0 -> x1, waiting for transfers between devices: none -> 91.3 us  [shards(): rows_in = lax.all_gather(normed, EP, axis=0, tiled=True)]
    all_gather x0 -> x1, blocking collectives: none -> 78 us  [shards(): weights = lax.all_gather(weight.T, EP, axis=1, tiled=True)]
    select_n x2 -> x0, local copies, waits for them, and re-layouts: 22.6 us -> none  [shards(): jnp.where(upper, jnp.concatenate([partner, received], axis=1), jnp.concat...]
    select_n x3 -> x0, other arithmetic: 22.2 us -> none  [the longest x2 13.7 us: shards(): jnp.where(upper, jnp.concatenate([partner, received], axis=1), jnp.concat...]
  transfers between devices with their start and end apart: 5 -> 2, of which waited for: 5 -> 2; matrix products, arithmetic and copies ran while one was open for 0% -> 1% of each run, Pallas kernels for 0% -> 0%
where the time goes in v1:
time: 476 us; the launch traced here: 475 us
  waiting for transfers between devices  330 us (69%)
  blocking collectives  78 us (16%)
  matrix products  46.7 us (10%)
  between operations  13.5 us (3%)
  other arithmetic  7.22 us (2%)
    reduce_scatter x1, waiting for transfers between devices, shards(): mixture = lax.psum_scatter(share, EP, scatter_dimension=0, tiled=True)  238 us
    all_gather x1, waiting for transfers between devices, shards(): rows_in = lax.all_gather(normed, EP, axis=0, tiled=True)  91.3 us
    all_gather x1, blocking collectives, shards(): weights = lax.all_gather(weight.T, EP, axis=1, tiled=True)  78 us
    dot_general x1, matrix products, shards(): jnp.dot(rows_in, gate_up_weight[0], preferred_element_type=jnp.float32)  24.6 us
    dot_general x1, matrix products, shards(): jnp.dot(activated, down_weight[0], preferred_element_type=jnp.float32)  20.9 us
  transfers between devices with their start and end apart: 2, of which 2 were waited for; matrix products, arithmetic and copies ran while one was open for 1% of the time, Pallas kernels for 0%

profile of v1, /device:TPU:46, one launch (start us, length us, event | category | flops | bytes accessed | tf_op | source)
XLA Modules:
  0.0 475.4 jit_solution(5916361895588588563)
XLA Ops:
  6.5 0.0 copy-start
  6.6 0.0 all-gather.3.cloned.1.call-start
  6.6 0.8 convert_element_type.22
  7.4 1.2 fusion.9
  8.6 1.9 fusion.11
  10.5 0.1 all-gather.3.cloned.1.call-update
  10.5 0.1 reduce-scatter.2.cloned.1.call-start
  10.6 1.2 fusion.15
  11.8 0.7 select_reduce_fusion.1
  12.6 0.7 select_reduce_fusion
  13.3 78.0 %all-gather = f32[64,64,16]{1,2,0:T(8,128)S(1)} all-gather(f32[1,64,16]{1,2,0:T(8,128)S(1)} %bitcast.15), channel_id=1, replica_groups=mesh['groups'=4,'ep_0'=32,'ep_1'=2] {'ep_0','ep_1'}, dimensions={0}, use_global_device_ids=true | all-gather | bytes 266240 | tf_op jit(solution)/shard_map/all_gather | solution.py:29
  91.3 0.2 copy.16
  91.5 0.2 reshape.43
  91.7 91.3 %all-gather.3.cloned.1.call-done = bf16[4096,2880]{1,0:T(8,128)(2,1)} async-done(((bf16[64,2880]{1,0:T(8,128)(2,1)}), bf16[4096,2880]{1,0:T(8,128)(2,1)}) %all-gather.3.cloned.1.call-update) | async-done | bytes 23592976 | tf_op jit(solution)/shard_map/all_gather | solution.py:21
  183.0 24.6 %fusion.3 = f32[4096,720]{0,1:T(8,128)} fusion(bf16[4096,2880]{1,0:T(8,128)(2,1)} %all-gather.3.cloned.1.call-done, bf16[1,2880,720]{1,2,0:T(8,128)(2,1)} %param.10), kind=kOutput, calls=%fused_computation.5 | convolution fusion | flops 16986931200 | bytes 39536640 | tf_op jit(solution)/shard_map/dot_general | solution.py:32
  207.6 0.0 copy-done
  207.6 20.9 %select_convert_fusion = bf16[4096,2880]{1,0:T(8,128)(2,1)} fusion(f32[4096]{0:T(1024)S(1)} %bitcast.14, pred[4096]{0:T(1024)(128)(4,1)S(1)} %broadcast_compare_fusion, f32[4096,720]{0,1:T(8,128)} %fusion.3, bf16[1,360,2880]{2,1,0:T(8,128)(2,1)S(1)} %copy-done), kind=kOutput, calls=%fused_computation | convolution fusion | flops 8540651520 | bytes 37483520 | tf_op jit(solution)/shard_map/dot_general | solution.py:38
  228.5 0.0 copy-start.2
  228.5 0.1 reduce-scatter.2.cloned.1.call-update
  228.6 0.0 copy-start.1
  228.6 238.1 %reduce-scatter.2.cloned.1.call-done = bf16[64,2880]{1,0:T(8,128)(2,1)} async-done(((bf16[4096,2880]{1,0:T(8,128)(2,1)}), bf16[64,2880]{1,0:T(8,128)(2,1)}) %reduce-scatter.2.cloned.1.call-update) | async-done | bytes 368656 | tf_op jit(solution)/shard_map/reduce_scatter | solution.py:40
  466.7 0.0 copy-done.2
  466.7 1.8 fusion.12
  468.6 0.0 copy-done.1
  (5 shorter events, 0.1 us)
Async XLA Ops:
  6.5 201.1 %copy-start = (bf16[1,360,2880]{2,1,0:T(8,128)(2,1)S(1)}, bf16[1,360,2880]{2,1,0:T(8,128)(2,1)}, u32[]{:S(2)}) copy-start(bf16[1,360,2880]{2,1,0:T(8,128)(2,1)} %param.11) | copy-start | bytes 6220804
  6.6 176.5 %all-gather.3.cloned.1.call-start = ((), (), s32[]{:S(2)}) async-start(), calls=%async_computation.1 | async-start | bytes 24494080 | tf_op jit(solution)/shard_map/all_gather | solution.py:21
  10.5 456.2 %reduce-scatter.2.cloned.1.call-start = ((), (), s32[]{:S(2)}) async-start(), calls=%async_computation.2 | async-start | bytes 24494080 | tf_op jit(solution)/shard_map/reduce_scatter | solution.py:40
  228.5 238.2 %copy-start.2 = (bf16[64,2880]{1,0:T(8,128)(2,1)S(1)}, bf16[64,2880]{1,0:T(8,128)(2,1)}, u32[]{:S(2)}) copy-start(bf16[64,2880]{1,0:T(8,128)(2,1)} %param.6) | copy-start | bytes 1105924
  228.6 240.0 %copy-start.1 = (bf16[1,360,2880]{2,1,0:T(8,128)(2,1)S(1)}, bf16[1,360,2880]{2,1,0:T(8,128)(2,1)}, u32[]{:S(2)}) copy-start(bf16[1,360,2880]{2,1,0:T(8,128)(2,1)} %param.11) | copy-start | bytes 6220804
Sparse Core Ops, SparseCore 0:
  10.7 172.3 all-gather.2
  228.7 237.9 reduce-scatter.1

commit v2 on v1

v2 whole, which is shorter than its diff:
```python
import functools

import jax
import jax.numpy as jnp
from jax import lax
from jax.experimental import pallas as pl
from jax.experimental.pallas import tpu as pltpu
from jax.sharding import PartitionSpec as P

MESH = pl.DeviceIdType.MESH
CORES = 2
CHUNK = 16
DIRS = 2
F32, BF16 = jnp.float32, jnp.bfloat16


def reach_limits(tok_rows, top_count, experts, shard_count):
    capacity = min(
        tok_rows, shard_count * (17 * tok_rows * top_count // (16 * experts * shard_count) + 1)
    )
    half = experts // 2

    def chunks_at(hop):
        offset = (hop + 1) // 2
        return pl.cdiv(min(tok_rows, (half - offset + 1) * capacity), CHUNK)

    hops = range(1, 2 * half)
    return [max(h for h in hops if chunks_at(h) > q) for q in range(tok_rows // CHUNK)]


def kernel(
    limits,
    experts,
    shard_count,
    tokens_ref,
    routes_ref,
    gain_ref,
    router_ref,
    gate_up_ref,
    down_ref,
    out_ref,
    rows_buf,
    share_buf,
    back_buf,
    gate_up_buf,
    down_buf,
    act_buf,
    place_buf,
    local_sem,
    pair_send,
    pair_recv,
    go_send,
    go_recv,
    back_send,
    back_recv,
):
    chips = lax.axis_size("ep") // CORES
    last = chips // 2
    tok_rows, width = tokens_ref.shape
    top_count = routes_ref.shape[1]
    wide = rows_buf.shape[2]
    ff_dev = down_ref.shape[1]
    aligned = wide - 128
    me = lax.axis_index("ep")
    chip, core = me // CORES, me % CORES
    my_expert = me // shard_count
    sibling = chip * CORES + (1 - core)
    ahead = lax.rem(chip + 1, chips) * CORES + core
    behind = lax.rem(chip + chips - 1, chips) * CORES + core

    def to(device):
        return {"ep": device}

    own_copies = [
        pltpu.make_async_copy(gate_up_ref.at[0], gate_up_buf.at[0, pl.ds(0, width)], local_sem.at[0]),
        pltpu.make_async_copy(down_ref.at[0], down_buf.at[0], local_sem.at[1]),
    ]
    for copy in own_copies:
        copy.start()
    barrier = pltpu.get_barrier_semaphore()
    for device in (sibling, ahead, behind):
        pl.semaphore_signal(barrier, inc=1, device_id=to(device), device_id_type=MESH)

    stream = tokens_ref[...].astype(F32)
    mean_square = jnp.sum(stream * stream, axis=1, keepdims=True) / width
    normed = (stream * lax.rsqrt(mean_square + 1e-05) * gain_ref[...].astype(F32)).astype(BF16)
    logits = jnp.dot(normed, router_ref[...], preferred_element_type=F32)
    routes = routes_ref[...]
    expert_ids = lax.broadcasted_iota(jnp.int32, (tok_rows, experts), 1)
    picks = [routes[:, k : k + 1] == expert_ids for k in range(top_count)]
    expo = [
        jnp.exp(jnp.sum(jnp.where(pick, logits, 0.0), axis=1, keepdims=True)) for pick in picks
    ]
    total = expo[0]
    for value in expo[1:]:
        total = total + value
    weight = jnp.zeros((tok_rows, experts), F32)
    for pick, value in zip(picks, expo):
        weight = weight + jnp.where(pick, value / total, 0.0)

    high = weight.astype(BF16)
    rest = weight - high.astype(F32)
    middle = rest.astype(BF16)
    low = (rest - middle.astype(F32)).astype(BF16)
    tail_width = width - aligned

    def shift_to(start, count):
        source = lax.broadcasted_iota(jnp.int32, (count, 128), 0)
        target = lax.broadcasted_iota(jnp.int32, (count, 128), 1)
        return jnp.where(target == source + start, 1.0, 0.0).astype(BF16)

    tail = jnp.dot(normed[:, aligned:], shift_to(0, tail_width), preferred_element_type=F32)
    for place, piece in enumerate((high, middle, low)):
        tail = tail + jnp.dot(
            piece, shift_to(tail_width + place * experts, experts), preferred_element_type=F32
        )
    tail = tail.astype(BF16)

    row_id = lax.broadcasted_iota(jnp.int32, (tok_rows, tok_rows), 0)
    col_id = lax.broadcasted_iota(jnp.int32, (tok_rows, tok_rows), 1)
    half = experts // 2
    for way in range(DIRS):
        distance = routes - my_expert if way == 0 else my_expert - routes
        distance = jnp.where(distance < 0, distance + experts, distance)
        distance = jnp.where(distance <= half, distance, 0).astype(F32)
        key = jnp.max(distance, axis=1, keepdims=True)
        key_row = jnp.sum(jnp.where(row_id == col_id, key, 0.0), axis=0, keepdims=True)
        first = (key_row > key) | ((key_row == key) & (col_id < row_id))
        rank = jnp.sum(jnp.where(first, 1.0, 0.0), axis=1, keepdims=True)
        place_buf[way] = jnp.where(rank == col_id.astype(F32), 1.0, 0.0).astype(BF16)
        later = (key > key_row) | ((key == key_row) & (row_id < col_id))
        rank_row = jnp.sum(jnp.where(later, 1.0, 0.0), axis=0, keepdims=True)
        order = jnp.where(rank_row == row_id.astype(F32), 1.0, 0.0).astype(BF16)
        rows = pl.ds(way * tok_rows, tok_rows)
        rows_buf[0, rows, :aligned] = jnp.dot(
            order, normed[:, :aligned], preferred_element_type=F32
        ).astype(BF16)
        rows_buf[0, rows, aligned:] = jnp.dot(order, tail, preferred_element_type=F32).astype(BF16)
    spare = 1 - lax.rem(chip, 2)
    spare_rows = pl.ds(pl.multiple_of(spare * tok_rows, tok_rows), tok_rows)
    rows_buf[last, spare_rows, :] = rows_buf[0, spare_rows, :]
    for shard in range(CORES):
        gate_up_buf[shard, width:, :] = jnp.zeros(
            (gate_up_buf.shape[1] - width, gate_up_buf.shape[2]), BF16
        )

    def chunk_rows(way, q):
        return pl.ds(way * tok_rows + q * CHUNK, CHUNK)

    def go(way, hop, q):
        return pltpu.make_async_remote_copy(
            src_ref=rows_buf.at[hop - 1, chunk_rows(way, q)],
            dst_ref=rows_buf.at[hop, chunk_rows(way, q)],
            send_sem=go_send.at[way, hop - 1, q],
            recv_sem=go_recv.at[way, hop - 1, q],
            device_id=to(ahead if way == 0 else behind),
            device_id_type=MESH,
        )

    def back(way, hop, q):
        return pltpu.make_async_remote_copy(
            src_ref=share_buf.at[hop, chunk_rows(way, q)],
            dst_ref=back_buf.at[hop - 1, chunk_rows(way, q)],
            send_sem=back_send.at[way, hop - 1, q],
            recv_sem=back_recv.at[way, hop - 1, q],
            device_id=to(behind if way == 0 else ahead),
            device_id_type=MESH,
        )

    def limit(way, hop, q):
        odd = lax.rem(chip + hop, 2)
        return limits[q] + (1 - odd if way == 0 else odd)

    chunks = [(q, way) for q in range(len(limits)) for way in range(DIRS)]

    pl.semaphore_wait(barrier, 3)
    for q, way in chunks:
        go(way, 1, q).start()
    pair_copies = [
        pltpu.make_async_remote_copy(
            src_ref=source,
            dst_ref=target,
            send_sem=pair_send.at[at],
            recv_sem=pair_recv.at[at],
            device_id=to(sibling),
            device_id_type=MESH,
        )
        for at, (source, target) in enumerate(
            (
                (gate_up_ref.at[0], gate_up_buf.at[1, pl.ds(0, width)]),
                (down_ref.at[0], down_buf.at[1]),
            )
        )
    ]
    for copy in pair_copies:
        copy.start()

    def up_piece(slot, shard):
        hidden = jnp.dot(rows_buf[slot], gate_up_buf[shard], preferred_element_type=F32)
        gate = hidden[:, :ff_dev]
        up = hidden[:, ff_dev:]
        act_buf[shard] = ((up + 1.0) * gate * jax.nn.sigmoid(1.702 * gate)).astype(BF16)

    def down_piece(slot, start, stop):
        lane = lax.broadcasted_iota(jnp.int32, (DIRS * tok_rows, 128), 1)
        mine = (
            (lane == tail_width + my_expert)
            | (lane == tail_width + experts + my_expert)
            | (lane == tail_width + 2 * experts + my_expert)
        )
        parts = rows_buf[slot, :, aligned:].astype(F32)
        factor = jnp.sum(jnp.where(mine, parts, 0.0), axis=1, keepdims=True)
        value = jnp.dot(act_buf[0], down_buf[0, :, start:stop], preferred_element_type=F32)
        value = value + jnp.dot(act_buf[1], down_buf[1, :, start:stop], preferred_element_type=F32)
        share_buf[slot, :, start:stop] = jnp.where(factor != 0.0, value * factor, 0.0).astype(BF16)

    middle_column = 256 * (width // 512 + 1)

    def piece(slot, part):
        if part < CORES:
            up_piece(slot, part)
        elif part == CORES:
            down_piece(slot, 0, middle_column)
        else:
            down_piece(slot, middle_column, width)

    def gather_step(hop, carry):
        for q in range(len(limits)):
            for way in range(DIRS):
                bound = limit(way, hop, q)

                @pl.when(hop <= bound)
                def _():
                    go(way, hop, q).wait_recv()

                @pl.when(hop + 1 <= bound)
                def _():
                    go(way, hop + 1, q).start()

            if q < len(limits) - 1:

                @pl.when(hop >= 2)
                def _():
                    piece(hop - 1, q + 1)
            else:

                @pl.when(hop == 1)
                def _():
                    for copy in own_copies:
                        copy.wait()
                    for copy in pair_copies:
                        copy.wait_recv()

                @pl.when(hop <= last)
                def _():
                    piece(hop, 0)

        return carry

    lax.fori_loop(1, last + 2, gather_step, 0)

    def return_step(step, carry):
        hop = last - step
        for q in range(len(limits)):
            for way in range(DIRS):
                bound = limit(way, hop, q)
                rows = chunk_rows(way, q)

                @pl.when(hop + 1 <= bound)
                def _():
                    back(way, hop + 1, q).wait_recv()
                    share_buf[hop, rows, :] = (
                        share_buf[hop, rows, :].astype(F32) + back_buf[hop, rows, :].astype(F32)
                    ).astype(BF16)

            for way in range(DIRS):
                bound = limit(way, hop, q)

                @pl.when(hop <= bound)
                def _():
                    back(way, hop, q).start()

        return carry

    lax.fori_loop(0, last, return_step, 0)

    def drain_step(hop, carry):
        for q, way in chunks:
            @pl.when(hop + 1 <= limit(way, hop, q))
            def _():
                go(way, hop + 1, q).wait_send()

            @pl.when((hop >= 1) & (hop <= limit(way, hop, q)))
            def _():
                back(way, hop, q).wait_send()

        return carry

    for q, way in chunks:
        back(way, 1, q).wait_recv()
    own = jnp.where(spare == 0, place_buf[0].astype(F32), place_buf[1].astype(F32)).astype(BF16)
    mixture = jnp.dot(own, share_buf[last, spare_rows, :], preferred_element_type=F32)
    for way in range(DIRS):
        mixture = mixture + jnp.dot(
            place_buf[way],
            back_buf[0, pl.ds(way * tok_rows, tok_rows), :],
            preferred_element_type=F32,
        )
    out_ref[...] = (tokens_ref[...].astype(F32) + mixture).astype(out_ref.dtype)
    lax.fori_loop(0, last + 1, drain_step, 0)
    for copy in pair_copies:
        copy.wait_send()


def shards(tokens, routes, norm_gain, router_weight, gate_up_weight, down_weight):
    tok_rows, width = tokens.shape
    experts = router_weight.shape[1]
    devices = lax.axis_size("ep")
    shard_count = devices // experts
    chips = devices // CORES
    ff_dev = down_weight.shape[1]
    limits = reach_limits(tok_rows, routes.shape[1], experts, shard_count)
    wide = width + 64
    last = chips // 2
    vmem = pl.BlockSpec(memory_space=pltpu.VMEM)
    hbm = pl.BlockSpec(memory_space=pl.ANY)
    copies = pltpu.SemaphoreType.DMA((DIRS, last, len(limits)))
    return pl.pallas_call(
        functools.partial(kernel, limits, experts, shard_count),
        out_shape=jax.ShapeDtypeStruct((tok_rows, width), BF16),
        in_specs=[vmem, vmem, vmem, vmem, hbm, hbm],
        out_specs=vmem,
        scratch_shapes=[
            pltpu.VMEM((last + 1, DIRS * tok_rows, wide), BF16),
            pltpu.VMEM((last + 1, DIRS * tok_rows, width), BF16),
            pltpu.VMEM((last, DIRS * tok_rows, width), BF16),
            pltpu.VMEM((CORES, wide, 2 * ff_dev), BF16),
            pltpu.VMEM((CORES, ff_dev, width), BF16),
            pltpu.VMEM((CORES, DIRS * tok_rows, ff_dev), BF16),
            pltpu.VMEM((DIRS, tok_rows, tok_rows), BF16),
            pltpu.SemaphoreType.DMA((2,)),
            pltpu.SemaphoreType.DMA((2,)),
            pltpu.SemaphoreType.DMA((2,)),
            copies,
            copies,
            copies,
            copies,
        ],
        compiler_params=pltpu.CompilerParams(
            collective_id=0, has_side_effects=True, vmem_limit_bytes=60 * 1024 * 1024
        ),
    )(tokens, routes, norm_gain.reshape(1, width), router_weight, gate_up_weight, down_weight)


def solution(mesh):
    rows = P(("groups", "ep"), None)
    return jax.shard_map(
        shards,
        mesh=mesh,
        in_specs=(rows, rows, P(), P(), P("ep", None, None), P("ep", None, None)),
        out_specs=rows,
        check_vma=False,
    )
```

time: 476 us -> 290 us (0.61)
  waiting for transfers between devices: 330 us -> 0 us
  Pallas kernels: 0 us -> 277 us
  blocking collectives: 78 us -> 0 us
  matrix products: 46.7 us -> 0 us
  between operations: 13.5 us -> 0.01 us
  local copies, waits for them, and re-layouts: 0.39 us -> 13 us
  other arithmetic: 7.22 us -> 0 us
    pallas_call x0 -> x1, Pallas kernels: none -> 277 us  [shards(): pl.pallas_call(functools.partial(kernel, limits, experts, shard_count), o...]
    reduce_scatter x1 -> x0, waiting for transfers between devices: 238 us -> none  [shards(): mixture = lax.psum_scatter(share, EP, scatter_dimension=0, tiled=True)]
    all_gather x1 -> x0, waiting for transfers between devices: 91.3 us -> none  [shards(): rows_in = lax.all_gather(normed, EP, axis=0, tiled=True)]
    all_gather x1 -> x0, blocking collectives: 78 us -> none  [shards(): weights = lax.all_gather(weight.T, EP, axis=1, tiled=True)]
    dot_general x3 -> x0, matrix products: 46.7 us -> none  [the longest x1 24.6 us: shards(): jnp.dot(rows_in, gate_up_weight[0], preferred_element_type=jnp.float32)]
    unnamed x8 -> x4, local copies, waits for them, and re-layouts: 0.22 us -> 11.7 us
  transfers between devices with their start and end apart: 2 -> 0, of which waited for: 2 -> 0; matrix products, arithmetic and copies ran while one was open for 1% -> 0% of each run, Pallas kernels for 0% -> 0%
where the time goes in v2:
time: 290 us
  Pallas kernels  277 us (96%)
  local copies, waits for them, and re-layouts  13 us (4%)
    pallas_call x1, Pallas kernels, shards(): pl.pallas_call(functools.partial(kernel, limits, experts, shard_count), o...  277 us
    unnamed x4, local copies, waits for them, and re-layouts  11.7 us

profile of v2, /device:TPU:46, one launch (start us, length us, event | category | flops | bytes accessed | tf_op | source)
XLA Modules:
  0.0 289.5 jit_solution(7690860902694138480)
XLA Ops:
  0.0 1.3 reshape.3.gain_ref
  1.3 1.4 copy.7.routes_ref
  2.7 2.0 copy.8.router_ref
  4.7 6.5 %copy.9.gate_up_ref = bf16[1,2880,720]{2,1,0:T(8,128)(2,1)} copy(bf16[1,2880,720]{1,2,0:T(8,128)(2,1)} %param.10) | data formatting | bytes 8294400 | tf_op args[4]
  11.2 276.5 %shard_map.64 = bf16[64,2880]{1,0:T(8,128)(2,1)} custom-call(bf16[64,2880]{1,0:T(8,128)(2,1)} %tokens_ref.1, s32[64,4]{1,0:T(8,128)} %copy.7.routes_ref, bf16[1,2880]{1,0:T(2,128)(2,1)} %reshape.3.gain_ref, bf16[2880,16]{1,0:T(8,128)(2,1)} %copy.8.router_ref, bf16[1,2880,720]{2,1,0:T(8,128)(2,1)} %copy.9.gate_up_ref, bf16[1,360,2880]{2,1,0:T(8,128)(2,1)} %down_ref.1), custom_call_target="tpu_custom_call" | custom-call | tf_op jit(solution)/shard_map/pallas_call | solution.py:328
  287.8 1.8 copy.11
